TPU v7x, 32 devices: a whole 2x2x4 slice. The times are simulated.
32 devices in a mesh: lat: 8 (over z, x), depth: 4 (over y, core).
Axes of the slice: x: 2, y: 2, z: 4, core: 2. Of those that a mesh axis runs over, the one named last changes fastest.
Arguments:
- surface: float32 [128, 4096], P('lat'), may hold values from -6 to 6
- velocity: float32 [2, 128, 4096], P(None, 'lat'), may hold values from -6 to 6
- block_map: int32 [128, 4096], P('lat'), may hold values from 0 to 15
- free_flags: int32 [128, 4096], P('lat'), may hold values 0 or 1
- block_rates: float32 [16], replicated, may hold values from 0.2 to 2
- previous_mesh: float32 [128, 64, 4096], P('lat', 'depth'), may hold values from -6 to 6
Outputs:
- new_surface: float32 [128, 4096], P('lat')
- mesh_field: float32 [128, 64, 4096], P('lat', 'depth')
- column_norm: float32 [128], P('lat')
All inputs are finite; a program needn't handle non-finite values. No bound on the sum of `free_flags` on one device may be relied on, other than what follows from the above.
Results may differ from a plain program's by a relative error of at most 0.00002.
Values sent between devices are 32-bit elements; how exact they have to be, the bound alone decides.
A program may use at most 64 MiB of HBM per device.

v0:
```python
import functools

import jax
import jax.numpy as jnp
from jax import lax
from jax.experimental import pallas as pl
from jax.experimental.pallas import tpu as pltpu
from jax.sharding import PartitionSpec as P

ITERS = 2
TIME_STEP = 0.5
RELAX_WEIGHT = 0.8
MESH = pl.DeviceIdType.MESH
PAD = 128
TILE = 8
WIDTH = 512
CHUNKS = 4
EARLY = 3
SURF, SHIFT, FIRST = 0, 1, 2


def lanes_beside(window, width):
    span = window.shape[1]
    left = pltpu.roll(window, 1, 1)[:, PAD : PAD + width]
    right = pltpu.roll(window, span - 1, 1)[:, PAD : PAD + width]
    return window[:, PAD : PAD + width], left, right


def kernel(
    lats,
    depths,
    surface,
    velocity,
    block_map,
    free_flags,
    rates,
    previous,
    new_surface,
    field,
    norm,
    surf,
    vel,
    blocks,
    flags,
    shift,
    first,
    second,
    squares,
    sums,
    others,
    local_sem,
    lat_send,
    lat_recv,
    depth_send,
    depth_recv,
    sum_send,
    sum_recv,
):
    rows, layers, columns = previous.shape
    lat = lax.axis_index("lat")
    depth = lax.axis_index("depth")
    total_layers = layers * depths
    blocks_count = rates.shape[0]
    steps = columns // WIDTH
    piece = columns // CHUNKS
    has_low, has_high = lat > 0, lat < lats - 1
    has_above, has_below = depth > 0, depth < depths - 1
    body_rows = pl.ds(TILE, rows)
    body_layers = pl.ds(TILE, layers)
    body_cols = pl.ds(PAD, columns)

    locals_ = [
        pltpu.make_async_copy(surface, surf.at[body_rows, body_cols], local_sem.at[0]),
        pltpu.make_async_copy(velocity, vel, local_sem.at[1]),
        pltpu.make_async_copy(block_map, blocks, local_sem.at[2]),
        pltpu.make_async_copy(free_flags, flags, local_sem.at[3]),
        pltpu.make_async_copy(
            previous, first.at[pl.ds(1, rows), body_layers, body_cols], local_sem.at[4]
        ),
    ]
    for copy in locals_:
        copy.start()

    barrier = pltpu.get_barrier_semaphore()

    def greet(target):
        pl.semaphore_signal(barrier, inc=1, device_id=target, device_id_type=MESH)

    low_id = {"lat": jnp.maximum(lat - 1, 0)}
    high_id = {"lat": jnp.minimum(lat + 1, lats - 1)}
    above_id = {"depth": jnp.maximum(depth - 1, 0)}
    below_id = {"depth": jnp.minimum(depth + 1, depths - 1)}

    pl.when(has_low)(lambda: greet(low_id))
    pl.when(has_high)(lambda: greet(high_id))
    for k in range(1, depths):
        greet({"depth": lax.rem(depth + k, depths)})
    peers = depths - 1 + has_low.astype(jnp.int32) + has_high.astype(jnp.int32)
    pl.semaphore_wait(barrier, peers)

    def lateral(side, slot, src, dst):
        return pltpu.make_async_remote_copy(
            src_ref=src,
            dst_ref=dst,
            send_sem=lat_send.at[side, slot],
            recv_sem=lat_recv.at[side, slot],
            device_id=high_id if side == 0 else low_id,
            device_id_type=MESH,
        )

    def vertical(side, slot, src, dst):
        return pltpu.make_async_remote_copy(
            src_ref=src,
            dst_ref=dst,
            send_sem=depth_send.at[side, slot],
            recv_sem=depth_recv.at[side, slot],
            device_id=below_id if side == 0 else above_id,
            device_id_type=MESH,
        )

    def piece_cols(k):
        return pl.ds(PAD + k * piece, piece)

    lat_sends = (has_high, has_low)
    lat_recvs = (has_low, has_high)
    depth_sends = (has_below, has_above)
    depth_recvs = (has_above, has_below)
    own_edge = (rows, 1)
    far_edge = (0, rows + 1)
    own_layer = (TILE + layers - 1, TILE)
    far_layer = (TILE - 1, TILE + layers)

    surf_copies = [
        lateral(
            side,
            SURF,
            surf.at[pl.ds((TILE + rows - 1, TILE)[side], 1), body_cols],
            surf.at[pl.ds((TILE - 1, TILE + rows)[side], 1), body_cols],
        )
        for side in (0, 1)
    ]
    shift_copies = [
        lateral(
            side,
            SHIFT,
            shift.at[pl.ds((TILE + rows - 1, TILE)[side], 1), :],
            shift.at[pl.ds((TILE - 1, TILE + rows)[side], 1), :],
        )
        for side in (0, 1)
    ]
    first_copies = [
        [
            lateral(
                side,
                FIRST + k,
                previous.at[(rows - 1, 0)[side], :, pl.ds(k * piece, piece)],
                first.at[far_edge[side], body_layers, piece_cols(k)],
            )
            for side in (0, 1)
        ]
        for k in range(CHUNKS)
    ]
    second_copies = [
        [
            lateral(
                side,
                FIRST + CHUNKS + k,
                second.at[own_edge[side], body_layers, piece_cols(k)],
                second.at[far_edge[side], body_layers, piece_cols(k)],
            )
            for side in (0, 1)
        ]
        for k in range(CHUNKS)
    ]
    layer_copies = [
        vertical(
            side,
            0,
            previous.at[:, pl.ds((layers - 1, 0)[side], 1), :],
            first.at[pl.ds(1, rows), pl.ds(far_layer[side], 1), body_cols],
        )
        for side in (0, 1)
    ]
    spans = (pl.ds(2, rows - 2), pl.ds(1, 1), pl.ds(rows, 1))
    later_layers = [
        [
            vertical(
                side,
                1 + j,
                second.at[span, pl.ds(own_layer[side], 1), body_cols],
                second.at[span, pl.ds(far_layer[side], 1), body_cols],
            )
            for side in (0, 1)
        ]
        for j, span in enumerate(spans)
    ]
    sum_copies = [
        pltpu.make_async_remote_copy(
            src_ref=sums,
            dst_ref=others.at[k - 1],
            send_sem=sum_send.at[k - 1],
            recv_sem=sum_recv.at[k - 1],
            device_id={"depth": lax.rem(depth + k, depths)},
            device_id_type=MESH,
        )
        for k in range(1, depths)
    ]

    locals_[0].wait()
    for side in (0, 1):
        pl.when(lat_sends[side])(surf_copies[side].start)
    for side in (0, 1):
        pl.when(depth_sends[side])(layer_copies[side].start)
    for k in range(EARLY):
        for side in (0, 1):
            pl.when(lat_sends[side])(first_copies[k][side].start)

    zero_tile = jnp.zeros((layers, PAD), jnp.float32)

    def clear_pads(r, carry):
        for buffer in (first, second):
            for start in (0, PAD + columns):
                buffer[r, body_layers, pl.ds(start, PAD)] = zero_tile
        return carry

    lax.fori_loop(1, rows + 1, clear_pads, 0)
    for start in (0, PAD + columns):
        surf[body_rows, pl.ds(start, PAD)] = jnp.zeros((rows, PAD), jnp.float32)
    squares[...] = jnp.zeros_like(squares)

    for side in (0, 1):

        @pl.when(jnp.logical_not(lat_recvs[side]))
        def _(side=side):
            surf[pl.ds((TILE - 1, TILE + rows)[side], 1), body_cols] = jnp.zeros(
                (1, columns), jnp.float32
            )
            shift[pl.ds((TILE - 1, TILE + rows)[side], 1), :] = jnp.zeros(
                (1, columns), jnp.float32
            )
            for buffer in (first, second):
                buffer[far_edge[side], body_layers, body_cols] = jnp.zeros(
                    (layers, columns), jnp.float32
                )

    for copy in locals_[1:4]:
        copy.wait()
    for side in (0, 1):
        pl.when(lat_recvs[side])(surf_copies[side].wait_recv)

    def advect(step, carry):
        c = pl.multiple_of(step * WIDTH, WIDTH)
        cols = pl.ds(c, WIDTH)
        inner = pl.ds(pl.multiple_of(c + PAD, PAD), WIDTH)
        middle, left, right = lanes_beside(surf[body_rows, pl.ds(c, WIDTH + 2 * PAD)], WIDTH)
        before = pltpu.roll(surf[pl.ds(0, rows + TILE), inner], 1, 0)[TILE:]
        after = pltpu.roll(surf[pl.ds(TILE, rows + TILE), inner], rows + TILE - 1, 0)[:rows]
        grad_rows = (after - before) * 0.5
        grad_cols = (right - left) * 0.5
        laplace = after + before + right + left - 4.0 * middle
        names = blocks[:, cols]
        rate = jnp.full(names.shape, rates[0], jnp.float32)
        for label in range(1, blocks_count):
            rate = jnp.where(names == label, rates[label], rate)
        tendency = -vel[0, :, cols] * grad_rows - vel[1, :, cols] * grad_cols + rate * laplace
        fresh = middle + TIME_STEP * flags[:, cols].astype(jnp.float32) * tendency
        new_surface[:, cols] = fresh
        shift[body_rows, cols] = fresh - middle
        return carry

    lax.fori_loop(0, steps, advect, 0)
    locals_[4].wait()
    for side in (0, 1):
        pl.when(lat_sends[side])(shift_copies[side].start)
    for k in range(EARLY, CHUNKS):
        for side in (0, 1):
            pl.when(lat_sends[side])(first_copies[k][side].start)

    for side in (0, 1):
        pl.when(depth_recvs[side])(layer_copies[side].wait_recv)

    def profile_of(index):
        return (total_layers - index).astype(jnp.float32) / total_layers

    base = depth * layers
    profile = profile_of(base + lax.broadcasted_iota(jnp.int32, (layers, PAD), 0))
    above_profile = profile_of(base - 1)
    below_profile = profile_of(base + layers)
    sublane = lax.broadcasted_iota(jnp.int32, (layers, WIDTH), 0)
    at_first = sublane == 0
    at_last = sublane == layers - 1
    above = pl.ds(TILE - 1, 1)
    below = pl.ds(TILE + layers, 1)

    def widen(r, c):
        inner = pl.ds(c + PAD, WIDTH)
        row_shift = jnp.broadcast_to(shift[pl.ds(TILE - 1 + r, 1), pl.ds(c, WIDTH)], (layers, WIDTH))
        wide_profile = jnp.concatenate([profile] * (WIDTH // PAD), axis=1)
        first[r, body_layers, inner] = first[r, body_layers, inner] + row_shift * wide_profile

    def relaxed(source, r, c, top, bottom):
        inner = pl.ds(c + PAD, WIDTH)
        middle, left, right = lanes_beside(
            source[r, body_layers, pl.ds(c, WIDTH + 2 * PAD)], WIDTH
        )
        upper = jnp.where(at_first, top, pltpu.roll(middle, 1, 0))
        lower = jnp.where(at_last, bottom, pltpu.roll(middle, layers - 1, 0))
        across = source[r - 1, body_layers, inner] + source[r + 1, body_layers, inner]
        neighbours = across + (left + right) + (upper + lower)
        return (1.0 - RELAX_WEIGHT) * middle + (RELAX_WEIGHT / 6.0) * neighbours

    def sweep_once(r, c):
        inner = pl.ds(c + PAD, WIDTH)
        row_shift = shift[pl.ds(TILE - 1 + r, 1), pl.ds(c, WIDTH)]
        top = jnp.where(has_above, first[r, above, inner] + row_shift * above_profile, row_shift)
        bottom = jnp.where(has_below, first[r, below, inner] + row_shift * below_profile, 0.0)
        second[r, body_layers, inner] = relaxed(first, r, c, top, bottom)

    def sweep_twice(r, c):
        inner = pl.ds(c + PAD, WIDTH)
        row_shift = shift[pl.ds(TILE - 1 + r, 1), pl.ds(c, WIDTH)]
        top = jnp.where(has_above, second[r, above, inner], row_shift)
        bottom = jnp.where(has_below, second[r, below, inner], 0.0)
        value = relaxed(second, r, c, top, bottom)
        field[r - 1, :, pl.ds(c, WIDTH)] = value
        power = value * value
        part = squares[r - 1]
        for top in range(0, layers, TILE):
            for start in range(0, WIDTH, PAD):
                part = part + power[top : top + TILE, start : start + PAD]
        squares[r - 1] = part

    def over(low, count, visit):
        def body(t, carry):
            for step in range(steps):
                visit(t, step * WIDTH)
            return carry

        lax.fori_loop(low, low + count, body, 0)

    over(1, rows, widen)
    over(2, rows - 2, sweep_once)
    for side in (0, 1):
        pl.when(depth_sends[side])(later_layers[0][side].start)

    per_piece = piece // WIDTH
    for side in (0, 1):
        pl.when(lat_recvs[side])(shift_copies[side].wait_recv)
    for k in range(CHUNKS):
        for side in (0, 1):

            @pl.when(lat_recvs[side])
            def _(side=side, k=k):
                first_copies[k][side].wait_recv()
                for j in range(per_piece):
                    widen(far_edge[side], k * piece + j * WIDTH)

            near = own_edge[1 - side]
            for j in range(per_piece):
                sweep_once(near, k * piece + j * WIDTH)
            pl.when(lat_sends[1 - side])(second_copies[k][1 - side].start)
    for j in (1, 2):
        for side in (0, 1):
            pl.when(depth_sends[side])(later_layers[j][side].start)

    for side in (0, 1):
        pl.when(depth_recvs[side])(later_layers[0][side].wait_recv)
    over(3, rows - 4, sweep_twice)
    over(2, 1, sweep_twice)
    over(rows - 1, 1, sweep_twice)
    for j in (1, 2):
        for side in (0, 1):
            pl.when(depth_recvs[side])(later_layers[j][side].wait_recv)
    for k in range(CHUNKS):
        for side in (0, 1):
            pl.when(lat_recvs[side])(second_copies[k][side].wait_recv)
            near = own_edge[1 - side]
            for j in range(per_piece):
                sweep_twice(near, k * piece + j * WIDTH)

    sums[...] = jnp.sum(squares[...], axis=1)
    for copy in sum_copies:
        copy.start()
    for side in (0, 1):
        for copy in [surf_copies[side], shift_copies[side]] + [
            group[k][side] for group in (first_copies, second_copies) for k in range(CHUNKS)
        ]:
            pl.when(lat_sends[side])(copy.wait_send)
        for copy in [layer_copies[side]] + [later_layers[j][side] for j in range(3)]:
            pl.when(depth_sends[side])(copy.wait_send)
    total = sums[...]
    for k, copy in enumerate(sum_copies):
        copy.wait_recv()
        total = total + others[k]
    column = jnp.sum(total, axis=1, keepdims=True)
    square = jnp.broadcast_to(column, (rows, norm.shape[1]))
    ids = lax.broadcasted_iota(jnp.int32, square.shape, 0)
    lanes = lax.broadcasted_iota(jnp.int32, square.shape, 1)
    flat = jnp.sum(jnp.where(ids == lanes, square, 0.0), axis=0, keepdims=True)
    norm[...] = jnp.broadcast_to(jnp.sqrt(flat / (total_layers * columns)), norm.shape)
    for copy in sum_copies:
        copy.wait_send()


def solution(mesh):
    lats, depths = mesh.shape["lat"], mesh.shape["depth"]

    def per_device(surface, velocity, block_map, free_flags, block_rates, previous_mesh):
        rows, layers, columns = previous_mesh.shape
        wide = columns + 2 * PAD
        anywhere = pl.BlockSpec(memory_space=pltpu.HBM)
        f32 = jnp.float32
        slots = 2 + 2 * CHUNKS
        others = max(depths - 1, 1)
        held = [
            pltpu.with_memory_space_constraint(value, pltpu.HBM)
            for value in (surface, velocity, block_map, free_flags, previous_mesh)
        ]
        new_surface, field, norm = pl.pallas_call(
            functools.partial(kernel, lats, depths),
            out_shape=(
                pltpu.VMEM(surface.shape, f32),
                pltpu.VMEM(previous_mesh.shape, f32),
                pltpu.VMEM((TILE, pl.cdiv(rows, PAD) * PAD), f32),
            ),
            in_specs=[anywhere] * 4 + [pl.BlockSpec(memory_space=pltpu.SMEM), anywhere],
            out_specs=(pl.BlockSpec(memory_space=pltpu.VMEM),) * 3,
            scratch_shapes=[
                pltpu.VMEM((rows + 2 * TILE, wide), f32),
                pltpu.VMEM(velocity.shape, f32),
                pltpu.VMEM(block_map.shape, jnp.int32),
                pltpu.VMEM(free_flags.shape, jnp.int32),
                pltpu.VMEM((rows + 2 * TILE, columns), f32),
                pltpu.VMEM((rows + 2, layers + 2 * TILE, wide), f32),
                pltpu.VMEM((rows + 2, layers + 2 * TILE, wide), f32),
                pltpu.VMEM((rows, TILE, PAD), f32),
                pltpu.VMEM((rows, PAD), f32),
                pltpu.VMEM((others, rows, PAD), f32),
                pltpu.SemaphoreType.DMA((5,)),
                pltpu.SemaphoreType.DMA((2, slots)),
                pltpu.SemaphoreType.DMA((2, slots)),
                pltpu.SemaphoreType.DMA((2, 4)),
                pltpu.SemaphoreType.DMA((2, 4)),
                pltpu.SemaphoreType.DMA((others,)),
                pltpu.SemaphoreType.DMA((others,)),
            ],
            compiler_params=pltpu.CompilerParams(
                collective_id=0, has_side_effects=True, vmem_limit_bytes=56 * 1024 * 1024
            ),
            name="advect_and_relax",
        )(*held[:4], block_rates, held[4])
        return new_surface, field, norm[0, :rows]

    return jax.shard_map(
        per_device,
        mesh=mesh,
        in_specs=(
            P("lat", None),
            P(None, "lat", None),
            P("lat", None),
            P("lat", None),
            P(),
            P("lat", "depth", None),
        ),
        out_specs=(P("lat", None), P("lat", "depth", None), P("lat")),
        check_vma=False,
    )
```

profile of v0, /device:TPU:11, one launch (start us, length us, event | category | flops | bytes accessed | tf_op | source)
XLA Modules:
  0.0 36.4 jit_solution(11024866910018130369)
XLA Ops:
  0.6 32.5 %advect_and_relax.1 = (f32[16,4096]{1,0:T(8,128)S(1)}, f32[16,16,4096]{2,1,0:T(8,128)S(1)}, f32[8,128]{1,0:T(8,128)S(1)}) custom-call(f32[16,4096]{1,0:T(8,128)} %surface.1, f32[2,16,4096]{2,1,0:T(8,128)} %velocity.1, s32[16,4096]{1,0:T(8,128)} %block_map.1, s32[16,4096]{1,0:T(8,128)} %free_flags.1, f32[16]{0:T(128)} %rates.1, f32[16,16,4096]{2,1,0:T(8,128)} %previous.1), custom_call_target="tpu_custom_call" | custom-call | tf_op jit(solution)/shard_map/advect_and_relax/pallas_call | solution.py:419
  33.2 0.7 %copy.11 = f32[16,4096]{1,0:T(8,128)} copy(f32[16,4096]{1,0:T(8,128)S(1)} %get-tuple-element.9) | data formatting | bytes 524288
  33.9 0.5 %slice_bitcast_fusion = f32[16]{0:T(128)} fusion(f32[8,128]{1,0:T(8,128)S(1)} %get-tuple-element.8), kind=kLoop, calls=%fused_computation | loop fusion | bytes 128 | tf_op jit(solution)/shard_map/squeeze | solution.py:452
  34.4 2.0 %copy.12 = f32[16,16,4096]{2,1,0:T(8,128)} copy(f32[16,16,4096]{2,1,0:T(8,128)S(1)} %get-tuple-element.10) | data formatting | bytes 8388608
where the time goes:
time: 36.6 us; the launch traced here: 36.4 us
  Pallas kernels  32.5 us (89%)
  local copies, waits for them, and re-layouts  3.23 us (9%)
  between operations  0.64 us (2%)
    pallas_call x1, Pallas kernels, per_device(): pl.pallas_call(functools.partial(kernel, lats, depths), out_shape=(pltpu....  32.5 us
    unnamed x2, local copies, waits for them, and re-layouts  2.72 us

commit v1 on v0

v1 whole, which is shorter than its diff:
```python
import functools

import jax
import jax.numpy as jnp
from jax import lax
from jax.experimental import pallas as pl
from jax.experimental.pallas import tpu as pltpu
from jax.sharding import PartitionSpec as P

ITERS = 2
TIME_STEP = 0.5
RELAX_WEIGHT = 0.8
SIDE_WEIGHT = RELAX_WEIGHT / 6.0
MESH = pl.DeviceIdType.MESH
PAD = 128
TILE = 8
WIDTH = 512
CHUNKS = 4
RAW = 2
PARTNER, OUTER = 0, 1


def lanes_beside(window, width):
    span = window.shape[1]
    left = pltpu.roll(window, 1, 1)[:, PAD : PAD + width]
    right = pltpu.roll(window, span - 1, 1)[:, PAD : PAD + width]
    return window[:, PAD : PAD + width], left, right


def kernel(
    lats,
    depths,
    surface,
    velocity,
    block_map,
    free_flags,
    rates,
    previous,
    new_surface,
    field,
    norm,
    surf,
    vel,
    blocks,
    flags,
    shift,
    first,
    second,
    mine,
    theirs,
    relay,
    squares,
    sums,
    others,
    local_sem,
    near_send,
    near_recv,
    plane_send,
    plane_recv,
    relay_recv,
    forward_send,
    depth_send,
    depth_recv,
    sum_send,
    sum_recv,
):
    rows, layers, columns = previous.shape
    lat = lax.axis_index("lat")
    depth = lax.axis_index("depth")
    total_layers = layers * depths
    blocks_count = rates.shape[0]
    steps = columns // WIDTH
    piece = columns // CHUNKS
    per_piece = piece // WIDTH
    has_low, has_high = lat > 0, lat < lats - 1
    has_above, has_below = depth > 0, depth < depths - 1
    body_rows = pl.ds(TILE, rows)
    body_layers = pl.ds(TILE, layers)
    body_cols = pl.ds(PAD, columns)
    raw_cols = pl.ds(0, RAW * piece)

    odd = lax.rem(lat, 2)
    pair, pairs = lat // 2, lats // 2
    partner = lat + 1 - 2 * odd
    outward = lat - 1 + 2 * odd
    beyond = lat + 2 - 4 * odd
    behind = lat - 2 + 4 * odd
    has_outer = jnp.logical_and(outward >= 0, outward < lats)
    has_beyond = jnp.logical_and(beyond >= 0, beyond < lats)
    down_share = (2 * CHUNKS * pair) // pairs
    up_share = (2 * CHUNKS * (pairs - 1 - pair)) // pairs
    own_share = jnp.where(odd == 0, down_share, up_share)
    relay_share = jnp.where(odd == 0, up_share, down_share)
    low_side, high_side = odd, 1 - odd
    edges = (1 + (rows - 1) * high_side, 1 + (rows - 1) * low_side)
    inners = (2 + (rows - 3) * high_side, 2 + (rows - 3) * low_side)
    halos = ((rows + 1) * high_side, (rows + 1) * low_side)

    locals_ = [
        pltpu.make_async_copy(surface, surf.at[body_rows, body_cols], local_sem.at[0]),
        pltpu.make_async_copy(velocity, vel, local_sem.at[1]),
        pltpu.make_async_copy(block_map, blocks, local_sem.at[2]),
        pltpu.make_async_copy(free_flags, flags, local_sem.at[3]),
        pltpu.make_async_copy(
            previous, first.at[pl.ds(1, rows), body_layers, body_cols], local_sem.at[4]
        ),
    ]
    barrier = pltpu.get_barrier_semaphore()

    def greet(target):
        pl.semaphore_signal(barrier, inc=1, device_id=target, device_id_type=MESH)

    def lat_id(index):
        return {"lat": jnp.clip(index, 0, lats - 1)}

    greet(lat_id(partner))
    pl.when(has_outer)(lambda: greet(lat_id(outward)))
    pl.when(has_beyond)(lambda: greet(lat_id(beyond)))
    pl.when(has_outer)(lambda: greet(lat_id(behind)))
    for k in range(1, depths):
        greet({"depth": lax.rem(depth + k, depths)})
    for copy in locals_:
        copy.start()
    peers = depths + 2 * has_outer.astype(jnp.int32) + has_beyond.astype(jnp.int32)
    with jax.named_scope("p01_barrier"):
        pl.semaphore_wait(barrier, peers)

    def remote(src, dst, send, recv, target):
        return pltpu.make_async_remote_copy(
            src_ref=src,
            dst_ref=dst,
            send_sem=send,
            recv_sem=recv,
            device_id=target,
            device_id_type=MESH,
        )

    def nearby(side, slot, src, dst):
        target = lat_id(lat + 1 if side == 0 else lat - 1)
        return remote(src, dst, near_send.at[side, slot], near_recv.at[side, slot], target)

    def vertical(side, slot, src, dst):
        index = depth + 1 if side == 0 else depth - 1
        target = {"depth": jnp.clip(index, 0, depths - 1)}
        return remote(src, dst, depth_send.at[side, slot], depth_recv.at[side, slot], target)

    def piece_cols(k, pad=0):
        return pl.ds(pad + k * piece, piece)

    lat_sends = (has_high, has_low)
    lat_recvs = (has_low, has_high)
    depth_sends = (has_below, has_above)
    depth_recvs = (has_above, has_below)
    own_layer = (TILE + layers - 1, TILE)
    far_layer = (TILE - 1, TILE + layers)
    own_row = (TILE + rows - 1, TILE)
    far_row = (TILE - 1, TILE + rows)

    surf_copies = [
        nearby(
            side,
            0,
            surface.at[pl.ds((rows - 1, 0)[side], 1), :],
            surf.at[pl.ds(far_row[side], 1), body_cols],
        )
        for side in (0, 1)
    ]
    shift_copies = [
        nearby(
            side,
            1,
            shift.at[pl.ds(own_row[side], 1), raw_cols],
            shift.at[pl.ds(far_row[side], 1), raw_cols],
        )
        for side in (0, 1)
    ]

    def source(flow, c):
        if c < RAW:
            return previous.at[edges[flow] - 1, :, piece_cols(c)]
        if c < CHUNKS:
            return first.at[edges[flow], body_layers, piece_cols(c, PAD)]
        return mine.at[flow, :, piece_cols(c - CHUNKS)]

    def landing(flow, halo, c):
        if c < CHUNKS:
            return first.at[halo, body_layers, piece_cols(c, PAD)]
        return theirs.at[flow, :, piece_cols(c - CHUNKS)]

    partner_halo = (rows + 1) * low_side
    outward_halo = (rows + 1) * high_side
    beyond_halo = (rows + 1) * low_side
    planes = range(2 * CHUNKS)
    partner_copies = [
        remote(
            source(PARTNER, c),
            landing(PARTNER, partner_halo, c),
            plane_send.at[PARTNER, c],
            plane_recv.at[PARTNER, c],
            lat_id(partner),
        )
        for c in planes
    ]
    outward_copies = [
        remote(
            source(OUTER, c),
            landing(OUTER, outward_halo, c),
            plane_send.at[OUTER, c],
            plane_recv.at[OUTER, c],
            lat_id(outward),
        )
        for c in planes
    ]
    detour_copies = [
        remote(
            source(OUTER, c),
            relay.at[c],
            plane_send.at[OUTER, c],
            relay_recv.at[c],
            lat_id(partner),
        )
        for c in planes
    ]
    forward_copies = [
        remote(
            relay.at[c],
            landing(OUTER, beyond_halo, c),
            forward_send.at[c],
            plane_recv.at[OUTER, c],
            lat_id(beyond),
        )
        for c in planes
    ]

    def send_outer(c):
        pl.when(own_share > c)(detour_copies[c].start)
        pl.when(jnp.logical_and(has_outer, own_share <= c))(outward_copies[c].start)

    def forward(c):
        @pl.when(relay_share > c)
        def _():
            detour_copies[c].wait_recv()
            forward_copies[c].start()

    spans = (pl.ds(1, 1), pl.ds(rows, 1), pl.ds(2, rows - 2))
    raw_spans = (pl.ds(0, 1), pl.ds(rows - 1, 1), pl.ds(1, rows - 2))
    raw_layers = [
        [
            vertical(
                side,
                j,
                previous.at[raw, pl.ds((layers - 1, 0)[side], 1), :],
                first.at[span, pl.ds(far_layer[side], 1), body_cols],
            )
            for side in (0, 1)
        ]
        for j, (raw, span) in enumerate(zip(raw_spans, spans))
    ]
    later_layers = [
        [
            vertical(
                side,
                3 + j,
                second.at[span, pl.ds(own_layer[side], 1), body_cols],
                second.at[span, pl.ds(far_layer[side], 1), body_cols],
            )
            for side in (0, 1)
        ]
        for j, span in enumerate(spans)
    ]
    sum_copies = [
        remote(
            sums,
            others.at[k - 1],
            sum_send.at[k - 1],
            sum_recv.at[k - 1],
            {"depth": lax.rem(depth + k, depths)},
        )
        for k in range(1, depths)
    ]

    def start_layers(group):
        for side in (0, 1):
            pl.when(depth_sends[side])(group[side].start)

    def wait_layers(group):
        for side in (0, 1):
            pl.when(depth_recvs[side])(group[side].wait_recv)

    def send(c):
        send_outer(c)
        partner_copies[c].start()

    with jax.named_scope("p02_sends"):
        for side in (0, 1):
            pl.when(lat_sends[side])(surf_copies[side].start)
        send(0)
        for group in raw_layers[:2]:
            start_layers(group)
        send(1)
        start_layers(raw_layers[2])

    zero_tile = jnp.zeros((layers, PAD), jnp.float32)

    def clear_pads(r, carry):
        for buffer in (first, second):
            for start in (0, PAD + columns):
                buffer[r, body_layers, pl.ds(start, PAD)] = zero_tile
        return carry

    lax.fori_loop(1, rows + 1, clear_pads, 0)
    for start in (0, PAD + columns):
        surf[body_rows, pl.ds(start, PAD)] = jnp.zeros((rows, PAD), jnp.float32)
    squares[...] = jnp.zeros_like(squares)

    for side in (0, 1):

        @pl.when(jnp.logical_not(lat_recvs[side]))
        def _(side=side):
            surf[pl.ds(far_row[side], 1), body_cols] = jnp.zeros((1, columns), jnp.float32)
            shift[pl.ds(far_row[side], 1), :] = jnp.zeros((1, columns), jnp.float32)
            first[(0, rows + 1)[side], body_layers, body_cols] = jnp.zeros(
                (layers, columns), jnp.float32
            )
            theirs[OUTER] = jnp.zeros((layers, columns), jnp.float32)

    with jax.named_scope("p04_waitsurf"):
        for copy in locals_[:4]:
            copy.wait()
        for side in (0, 1):
            pl.when(lat_recvs[side])(surf_copies[side].wait_recv)

    def advect(step, carry):
        c = pl.multiple_of(step * WIDTH, WIDTH)
        cols = pl.ds(c, WIDTH)
        inner = pl.ds(pl.multiple_of(c + PAD, PAD), WIDTH)
        middle, left, right = lanes_beside(surf[body_rows, pl.ds(c, WIDTH + 2 * PAD)], WIDTH)
        before = pltpu.roll(surf[pl.ds(0, rows + TILE), inner], 1, 0)[TILE:]
        after = pltpu.roll(surf[pl.ds(TILE, rows + TILE), inner], rows + TILE - 1, 0)[:rows]
        grad_rows = (after - before) * 0.5
        grad_cols = (right - left) * 0.5
        laplace = after + before + right + left - 4.0 * middle
        names = blocks[:, cols]
        rate = jnp.full(names.shape, rates[0], jnp.float32)
        for label in range(1, blocks_count):
            rate = jnp.where(names == label, rates[label], rate)
        tendency = -vel[0, :, cols] * grad_rows - vel[1, :, cols] * grad_cols + rate * laplace
        fresh = middle + TIME_STEP * flags[:, cols].astype(jnp.float32) * tendency
        new_surface[:, cols] = fresh
        shift[body_rows, cols] = fresh - middle
        return carry

    with jax.named_scope("p05_advect"):
        lax.fori_loop(0, steps, advect, 0)
    with jax.named_scope("p06_sends"):
        for side in (0, 1):
            pl.when(lat_sends[side])(shift_copies[side].start)
        locals_[4].wait()

    def profile_of(index):
        return (total_layers - index).astype(jnp.float32) / total_layers

    base = depth * layers
    profile = profile_of(base + lax.broadcasted_iota(jnp.int32, (layers, PAD), 0))
    above_profile = profile_of(base - 1)
    below_profile = profile_of(base + layers)
    sublane = lax.broadcasted_iota(jnp.int32, (layers, WIDTH), 0)
    at_first = sublane == 0
    at_last = sublane == layers - 1
    above = pl.ds(TILE - 1, 1)
    below = pl.ds(TILE + layers, 1)

    def widen(r, c):
        inner = pl.ds(c + PAD, WIDTH)
        row_shift = jnp.broadcast_to(shift[pl.ds(TILE - 1 + r, 1), pl.ds(c, WIDTH)], (layers, WIDTH))
        wide_profile = jnp.concatenate([profile] * (WIDTH // PAD), axis=1)
        first[r, body_layers, inner] = first[r, body_layers, inner] + row_shift * wide_profile

    def in_plane(source, r, c, top, bottom):
        middle, left, right = lanes_beside(
            source[r, body_layers, pl.ds(c, WIDTH + 2 * PAD)], WIDTH
        )
        upper = jnp.where(at_first, top, pltpu.roll(middle, 1, 0))
        lower = jnp.where(at_last, bottom, pltpu.roll(middle, layers - 1, 0))
        return middle, (left + right) + (upper + lower)

    def first_ends(r, c):
        inner = pl.ds(c + PAD, WIDTH)
        row_shift = shift[pl.ds(TILE - 1 + r, 1), pl.ds(c, WIDTH)]
        top = jnp.where(has_above, first[r, above, inner] + row_shift * above_profile, row_shift)
        bottom = jnp.where(has_below, first[r, below, inner] + row_shift * below_profile, 0.0)
        return top, bottom

    def second_ends(r, c):
        inner = pl.ds(c + PAD, WIDTH)
        row_shift = shift[pl.ds(TILE - 1 + r, 1), pl.ds(c, WIDTH)]
        top = jnp.where(has_above, second[r, above, inner], row_shift)
        bottom = jnp.where(has_below, second[r, below, inner], 0.0)
        return top, bottom

    def weigh(middle, neighbours):
        return (1.0 - RELAX_WEIGHT) * middle + SIDE_WEIGHT * neighbours

    def partial(flow, c):
        inner = pl.ds(c + PAD, WIDTH)
        middle, around = in_plane(first, edges[flow], c, *first_ends(edges[flow], c))
        mine[flow, :, pl.ds(c, WIDTH)] = weigh(
            middle, around + first[inners[flow], body_layers, inner]
        )

    def complete(flow, c):
        inner = pl.ds(c + PAD, WIDTH)
        second[edges[flow], body_layers, inner] = (
            mine[flow, :, pl.ds(c, WIDTH)] + SIDE_WEIGHT * first[halos[flow], body_layers, inner]
        )

    def sweep_once(r, c):
        inner = pl.ds(c + PAD, WIDTH)
        middle, around = in_plane(first, r, c, *first_ends(r, c))
        across = first[r - 1, body_layers, inner] + first[r + 1, body_layers, inner]
        second[r, body_layers, inner] = weigh(middle, across + around)

    def tally(r, c, value):
        field[r - 1, :, pl.ds(c, WIDTH)] = value
        power = value * value
        part = squares[r - 1]
        for top in range(0, layers, TILE):
            for start in range(0, WIDTH, PAD):
                part = part + power[top : top + TILE, start : start + PAD]
        squares[r - 1] = part

    def sweep_twice(r, c):
        inner = pl.ds(c + PAD, WIDTH)
        middle, around = in_plane(second, r, c, *second_ends(r, c))
        across = second[r - 1, body_layers, inner] + second[r + 1, body_layers, inner]
        tally(r, c, weigh(middle, across + around))

    reach = (jnp.float32(SIDE_WEIGHT), jnp.where(has_outer, SIDE_WEIGHT, 0.0))

    def prepare(flow, c):
        inner = pl.ds(c + PAD, WIDTH)
        edge = edges[flow]
        middle, around = in_plane(second, edge, c, *second_ends(edge, c))
        around = around + second[inners[flow], body_layers, inner]
        facing_own = reach[flow] * first[edge, body_layers, inner]
        field[edge - 1, :, pl.ds(c, WIDTH)] = weigh(middle, around + facing_own)

    def finish(flow, c):
        cols = pl.ds(c, WIDTH)
        edge = edges[flow]
        tally(edge, c, field[edge - 1, :, cols] + SIDE_WEIGHT * theirs[flow, :, cols])

    def over(low, count, visit):
        def body(t, carry):
            for step in range(steps):
                visit(t, step * WIDTH)
            return carry

        lax.fori_loop(low, low + count, body, 0)

    with jax.named_scope("p07_widen"):
        over(1, 2, widen)
        over(rows - 1, 2, widen)
        send(2)
        send(3)
    with jax.named_scope("p08_waitraw"):
        for group in raw_layers[:2]:
            wait_layers(group)
    with jax.named_scope("p09_partial"):
        for flow in (OUTER, PARTNER):
            for step in range(steps):
                partial(flow, step * WIDTH)
    with jax.named_scope("p10_fwd0"):
        forward(0)
    with jax.named_scope("p11_widen"):
        over(3, rows - 4, widen)
        send(4)
    with jax.named_scope("p12_waitraw"):
        wait_layers(raw_layers[2])
    middle_row = rows // 2 + 1
    with jax.named_scope("p13_sweep1"):
        over(2, middle_row - 2, sweep_once)
    with jax.named_scope("p14_fwd1"):
        send(5)
        forward(1)
    with jax.named_scope("p15_sweep1"):
        over(middle_row, rows - middle_row, sweep_once)
        start_layers(later_layers[2])
    with jax.named_scope("p16_fwd2"):
        send(6)
        send(7)
        forward(2)
    with jax.named_scope("p17_waitshift"):
        for side in (0, 1):
            pl.when(lat_recvs[side])(shift_copies[side].wait_recv)
    for k in range(CHUNKS):
        if k == CHUNKS - 1:
            with jax.named_scope("p18_fwd3"):
                forward(3)
        for flow in (PARTNER, OUTER):

            def arrive(flow=flow, k=k):
                (partner_copies, outward_copies)[flow][k].wait_recv()
                for j in range(per_piece if k < RAW else 0):
                    widen(halos[flow], k * piece + j * WIDTH)

            with jax.named_scope(f"p18_{k}{'po'[flow]}"):
                if flow == PARTNER:
                    arrive()
                else:
                    pl.when(has_outer)(arrive)
            for j in range(per_piece):
                complete(flow, k * piece + j * WIDTH)
    with jax.named_scope("p19_edges"):
        for j in (0, 1):
            start_layers(later_layers[j])
    with jax.named_scope("p20_waitlater"):
        wait_layers(later_layers[2])
    with jax.named_scope("p22_sweep2"):
        over(2, rows - 2, sweep_twice)
    with jax.named_scope("p23_waitlater"):
        for j in (0, 1):
            wait_layers(later_layers[j])
    with jax.named_scope("p24_prepare"):
        for flow in (PARTNER, OUTER):
            for step in range(steps):
                prepare(flow, step * WIDTH)

    for k in range(CHUNKS):
        with jax.named_scope(f"p25_finish{k}"):
            forward(CHUNKS + k)
            for flow in (PARTNER, OUTER):
                if flow == PARTNER:
                    partner_copies[CHUNKS + k].wait_recv()
                else:
                    pl.when(has_outer)(outward_copies[CHUNKS + k].wait_recv)
                for j in range(per_piece):
                    finish(flow, k * piece + j * WIDTH)

    sums[...] = jnp.sum(squares[...], axis=1)
    for copy in sum_copies:
        copy.start()
    for side in (0, 1):
        for copy in (surf_copies[side], shift_copies[side]):
            pl.when(lat_sends[side])(copy.wait_send)
        for group in raw_layers + later_layers:
            pl.when(depth_sends[side])(group[side].wait_send)
    for c in planes:
        partner_copies[c].wait_send()
        pl.when(has_outer)(outward_copies[c].wait_send)
        pl.when(relay_share > c)(forward_copies[c].wait_send)
    with jax.named_scope("p27_waitsums"):
        for copy in sum_copies:
            copy.wait_recv()
        for copy in sum_copies:
            copy.wait_send()
    with jax.named_scope("p28_total"):
        total = sums[...]
        for k in range(depths - 1):
            total = total + others[k]
        norm[...] = total


def deliver(count, surface_in, field_in, total, surface_out, field_out, norm_out, packed, sem):
    copies = [
        pltpu.make_async_copy(field_in, field_out, sem.at[0]),
        pltpu.make_async_copy(surface_in, surface_out, sem.at[1]),
        pltpu.make_async_copy(packed, norm_out, sem.at[2]),
    ]
    for copy in copies[:2]:
        copy.start()
    rows, lanes = total.shape[0], pl.cdiv(total.shape[0], PAD) * PAD
    column = jnp.broadcast_to(jnp.sum(total[...], axis=1, keepdims=True), (rows, lanes))
    ids = lax.broadcasted_iota(jnp.int32, column.shape, 0)
    places = lax.broadcasted_iota(jnp.int32, column.shape, 1)
    flat = jnp.sum(jnp.where(ids == places, column, 0.0), axis=0, keepdims=True)
    packed[...] = jnp.sqrt(flat / count)[0, :rows]
    copies[2].start()
    for copy in copies:
        copy.wait()


def solution(mesh):
    lats, depths = mesh.shape["lat"], mesh.shape["depth"]

    def per_device(surface, velocity, block_map, free_flags, block_rates, previous_mesh):
        rows, layers, columns = previous_mesh.shape
        wide = columns + 2 * PAD
        anywhere = pl.BlockSpec(memory_space=pltpu.HBM)
        f32 = jnp.float32
        others = max(depths - 1, 1)
        dma = pltpu.SemaphoreType.DMA
        held = [
            pltpu.with_memory_space_constraint(value, pltpu.HBM)
            for value in (surface, velocity, block_map, free_flags, previous_mesh)
        ]
        results = pl.pallas_call(
            functools.partial(kernel, lats, depths),
            out_shape=(
                pltpu.VMEM(surface.shape, f32),
                pltpu.VMEM(previous_mesh.shape, f32),
                pltpu.VMEM((rows, PAD), f32),
            ),
            in_specs=[anywhere] * 4 + [pl.BlockSpec(memory_space=pltpu.SMEM), anywhere],
            out_specs=(pl.BlockSpec(memory_space=pltpu.VMEM),) * 3,
            scratch_shapes=[
                pltpu.VMEM((rows + 2 * TILE, wide), f32),
                pltpu.VMEM(velocity.shape, f32),
                pltpu.VMEM(block_map.shape, jnp.int32),
                pltpu.VMEM(free_flags.shape, jnp.int32),
                pltpu.VMEM((rows + 2 * TILE, columns), f32),
                pltpu.VMEM((rows + 2, layers + 2 * TILE, wide), f32),
                pltpu.VMEM((rows + 2, layers + 2 * TILE, wide), f32),
                pltpu.VMEM((2, layers, columns), f32),
                pltpu.VMEM((2, layers, columns), f32),
                pltpu.VMEM((2 * CHUNKS, layers, columns // CHUNKS), f32),
                pltpu.VMEM((rows, TILE, PAD), f32),
                pltpu.VMEM((rows, PAD), f32),
                pltpu.VMEM((others, rows, PAD), f32),
                dma((5,)),
                dma((2, 2)),
                dma((2, 2)),
                dma((2, 2 * CHUNKS)),
                dma((2, 2 * CHUNKS)),
                dma((2 * CHUNKS,)),
                dma((2 * CHUNKS,)),
                dma((2, 6)),
                dma((2, 6)),
                dma((others,)),
                dma((others,)),
            ],
            compiler_params=pltpu.CompilerParams(
                collective_id=0, has_side_effects=True, vmem_limit_bytes=56 * 1024 * 1024
            ),
            name="advect_and_relax",
        )(*held[:4], block_rates, held[4])
        resident = [pltpu.with_memory_space_constraint(value, pltpu.VMEM) for value in results]
        new_surface, field, norm = pl.pallas_call(
            functools.partial(deliver, layers * depths * columns),
            out_shape=(
                pltpu.HBM(surface.shape, f32),
                pltpu.HBM(previous_mesh.shape, f32),
                pltpu.HBM((rows,), f32),
            ),
            in_specs=[pl.BlockSpec(memory_space=pltpu.VMEM)] * 3,
            out_specs=(anywhere,) * 3,
            scratch_shapes=[pltpu.VMEM((rows,), f32), dma((3,))],
            compiler_params=pltpu.CompilerParams(vmem_limit_bytes=1024 * 1024),
            name="deliver",
        )(*resident)
        return new_surface, field, norm

    return jax.shard_map(
        per_device,
        mesh=mesh,
        in_specs=(
            P("lat", None),
            P(None, "lat", None),
            P("lat", None),
            P("lat", None),
            P(),
            P("lat", "depth", None),
        ),
        out_specs=(P("lat", None), P("lat", "depth", None), P("lat")),
        check_vma=False,
    )
```

time: 36.6 us -> 33.3 us (0.910)
  the two profiles are of different devices: /device:TPU:11 before, /device:TPU:0 now
where the time goes in v1:
time: 33.3 us; the launch traced here: 32.9 us
  Pallas kernels  32.2 us (97%)
  between operations  0.64 us (2%)
    pallas_call x1, Pallas kernels, per_device(): pl.pallas_call(functools.partial(kernel, lats, depths), out_shape=(pltpu....  30.1 us
    pallas_call x1, Pallas kernels, per_device(): pl.pallas_call(functools.partial(deliver, layers * depths * columns), out...  2.11 us

profile of v1, /device:TPU:0, one launch (start us, length us, event | category | flops | bytes accessed | tf_op | source)
XLA Modules:
  0.0 32.9 jit_solution(16694445022377529066)
XLA Ops:
  0.6 30.1 %advect_and_relax.1 = (f32[16,4096]{1,0:T(8,128)S(1)}, f32[16,16,4096]{2,1,0:T(8,128)S(1)}, f32[16,128]{1,0:T(8,128)S(1)}) custom-call(f32[16,4096]{1,0:T(8,128)} %surface.1, f32[2,16,4096]{2,1,0:T(8,128)} %velocity.1, s32[16,4096]{1,0:T(8,128)} %block_map.1, s32[16,4096]{1,0:T(8,128)} %free_flags.1, f32[16]{0:T(128)} %rates.1, f32[16,16,4096]{2,1,0:T(8,128)} %previous.1), custom_call_target="tpu_custom_call" | custom-call | tf_op jit(solution)/shard_map/advect_and_relax/pallas_call | solution.py:597
  30.8 2.1 %deliver.1 = (f32[16,4096]{1,0:T(8,128)}, f32[16,16,4096]{2,1,0:T(8,128)}, f32[16]{0:T(128)}) custom-call(f32[16,4096]{1,0:T(8,128)S(1)} %get-tuple-element.6.surface_in, f32[16,16,4096]{2,1,0:T(8,128)S(1)} %get-tuple-element.7.field_in, f32[16,128]{1,0:T(8,128)S(1)} %get-tuple-element.8.total), custom_call_target="tpu_custom_call" | custom-call | tf_op jit(solution)/shard_map/deliver/pallas_call | solution.py:638

commit v2 on v1

--- a/solution.py
+++ b/solution.py
@@ -14,9 +14,9 @@
 MESH = pl.DeviceIdType.MESH
 PAD = 128
 TILE = 8
-WIDTH = 512
+WIDTH = 1024
 CHUNKS = 4
-RAW = 2
+RAW = (2, CHUNKS)
 PARTNER, OUTER = 0, 1
 
 
@@ -49,12 +49,15 @@
     mine,
     theirs,
     relay,
+    relay_shift,
     squares,
     sums,
     others,
     local_sem,
     near_send,
     near_recv,
+    shift_send,
+    shift_recv,
     plane_send,
     plane_recv,
     relay_recv,
@@ -77,7 +80,6 @@
     body_rows = pl.ds(TILE, rows)
     body_layers = pl.ds(TILE, layers)
     body_cols = pl.ds(PAD, columns)
-    raw_cols = pl.ds(0, RAW * piece)
 
     odd = lax.rem(lat, 2)
     pair, pairs = lat // 2, lats // 2
@@ -96,15 +98,18 @@
     inners = (2 + (rows - 3) * high_side, 2 + (rows - 3) * low_side)
     halos = ((rows + 1) * high_side, (rows + 1) * low_side)
 
-    locals_ = [
-        pltpu.make_async_copy(surface, surf.at[body_rows, body_cols], local_sem.at[0]),
+    local_surface = pltpu.make_async_copy(
+        surface, surf.at[body_rows, body_cols], local_sem.at[0]
+    )
+    local_inputs = [
         pltpu.make_async_copy(velocity, vel, local_sem.at[1]),
         pltpu.make_async_copy(block_map, blocks, local_sem.at[2]),
         pltpu.make_async_copy(free_flags, flags, local_sem.at[3]),
-        pltpu.make_async_copy(
-            previous, first.at[pl.ds(1, rows), body_layers, body_cols], local_sem.at[4]
-        ),
-    ]
+    ]
+    local_mesh = pltpu.make_async_copy(
+        previous, first.at[pl.ds(1, rows), body_layers, body_cols], local_sem.at[4]
+    )
+
     barrier = pltpu.get_barrier_semaphore()
 
     def greet(target):
@@ -119,7 +124,7 @@
     pl.when(has_outer)(lambda: greet(lat_id(behind)))
     for k in range(1, depths):
         greet({"depth": lax.rem(depth + k, depths)})
-    for copy in locals_:
+    for copy in [local_surface, *local_inputs, local_mesh]:
         copy.start()
     peers = depths + 2 * has_outer.astype(jnp.int32) + has_beyond.astype(jnp.int32)
     with jax.named_scope("p01_barrier"):
@@ -135,14 +140,14 @@
             device_id_type=MESH,
         )
 
-    def nearby(side, slot, src, dst):
+    def nearby(side, src, dst):
         target = lat_id(lat + 1 if side == 0 else lat - 1)
-        return remote(src, dst, near_send.at[side, slot], near_recv.at[side, slot], target)
+        return remote(src, dst, near_send.at[side], near_recv.at[side], target)
 
     def vertical(side, slot, src, dst):
         index = depth + 1 if side == 0 else depth - 1
         target = {"depth": jnp.clip(index, 0, depths - 1)}
-        return remote(src, dst, depth_send.at[side, slot], depth_recv.at[side, slot], target)
+        return remote(src, dst, depth_send.at[side], depth_recv.at[side, slot], target)
 
     def piece_cols(k, pad=0):
         return pl.ds(pad + k * piece, piece)
@@ -159,24 +164,60 @@
     surf_copies = [
         nearby(
             side,
-            0,
-            surface.at[pl.ds((rows - 1, 0)[side], 1), :],
+            surf.at[pl.ds(own_row[side], 1), body_cols],
             surf.at[pl.ds(far_row[side], 1), body_cols],
         )
         for side in (0, 1)
     ]
-    shift_copies = [
-        nearby(
-            side,
-            1,
-            shift.at[pl.ds(own_row[side], 1), raw_cols],
-            shift.at[pl.ds(far_row[side], 1), raw_cols],
+
+    def shift_row(row, flow):
+        return shift.at[pl.ds(row, 1), pl.ds(0, RAW[flow] * piece)]
+
+    shift_partner = [
+        remote(
+            shift_row(own_row[side], PARTNER),
+            shift_row(far_row[side], PARTNER),
+            shift_send.at[0],
+            shift_recv.at[0],
+            lat_id(partner),
         )
         for side in (0, 1)
     ]
+    shift_detour = [
+        remote(
+            shift_row(own_row[side], OUTER),
+            relay_shift,
+            shift_send.at[1],
+            shift_recv.at[1],
+            lat_id(partner),
+        )
+        for side in (0, 1)
+    ]
+    shift_forward = [
+        remote(
+            relay_shift,
+            shift_row(far_row[side], OUTER),
+            shift_send.at[2],
+            shift_recv.at[2],
+            lat_id(beyond),
+        )
+        for side in (0, 1)
+    ]
+
+    def send_shift():
+        for side in (0, 1):
+            toward = (odd == 0) if side == 0 else (odd == 1)
+            away = jnp.logical_and(has_outer, (odd == 1) if side == 0 else (odd == 0))
+            pl.when(away)(shift_detour[side].start)
+            pl.when(toward)(shift_partner[side].start)
+
+    def forward_shift():
+        shift_detour[0].wait_recv()
+        for side in (0, 1):
+            pl.when((odd == 0) if side == 0 else (odd == 1))(shift_forward[side].start)
 
     def source(flow, c):
-        if c < RAW:
+        if c < RAW[flow]:
             return previous.at[edges[flow] - 1, :, piece_cols(c)]
         if c < CHUNKS:
             return first.at[edges[flow], body_layers, piece_cols(c, PAD)]
@@ -190,54 +231,74 @@
     partner_halo = (rows + 1) * low_side
     outward_halo = (rows + 1) * high_side
     beyond_halo = (rows + 1) * low_side
-    planes = range(2 * CHUNKS)
+    pieces = range(2 * CHUNKS)
+    order = list(pieces)
+    most = (2 * CHUNKS * (pairs - 1)) // pairs
+    detours = order[:most]
+
+    def landed(flow, c):
+        return plane_recv.at[flow, max(c - CHUNKS + 1, 0)]
+
     partner_copies = [
         remote(
             source(PARTNER, c),
             landing(PARTNER, partner_halo, c),
-            plane_send.at[PARTNER, c],
-            plane_recv.at[PARTNER, c],
+            plane_send.at[PARTNER],
+            landed(PARTNER, c),
             lat_id(partner),
         )
-        for c in planes
+        for c in pieces
     ]
     outward_copies = [
         remote(
             source(OUTER, c),
             landing(OUTER, outward_halo, c),
-            plane_send.at[OUTER, c],
-            plane_recv.at[OUTER, c],
+            plane_send.at[OUTER],
+            landed(OUTER, c),
             lat_id(outward),
         )
-        for c in planes
-    ]
-    detour_copies = [
-        remote(
+        for c in pieces
+    ]
+    detour_copies = {
+        c: remote(
             source(OUTER, c),
-            relay.at[c],
-            plane_send.at[OUTER, c],
-            relay_recv.at[c],
+            relay.at[slot],
+            plane_send.at[OUTER],
+            relay_recv.at[slot],
             lat_id(partner),
         )
-        for c in planes
-    ]
-    forward_copies = [
-        remote(
-            relay.at[c],
+        for slot, c in enumerate(detours)
+    }
+    forward_copies = {
+        c: remote(
+            relay.at[slot],
             landing(OUTER, beyond_halo, c),
-            forward_send.at[c],
-            plane_recv.at[OUTER, c],
+            forward_send.at[0],
+            landed(OUTER, c),
             lat_id(beyond),
         )
-        for c in planes
-    ]
-
-    def send_outer(c):
-        pl.when(own_share > c)(detour_copies[c].start)
-        pl.when(jnp.logical_and(has_outer, own_share <= c))(outward_copies[c].start)
+        for slot, c in enumerate(detours)
+    }
+
+    def whole_plane(flow):
+        whole = first.at[halos[flow], body_layers, body_cols]
+        return remote(whole, whole, plane_send.at[flow], plane_recv.at[flow, 0], lat_id(partner))
+
+    def send_detour(c):
+        if c in detour_copies:
+            pl.when(own_share > detours.index(c))(detour_copies[c].start)
+
+    def send_direct(c):
+        direct = has_outer
+        if c in detour_copies:
+            direct = jnp.logical_and(has_outer, own_share <= detours.index(c))
+        pl.when(direct)(outward_copies[c].start)
 
     def forward(c):
-        @pl.when(relay_share > c)
+        if c not in forward_copies:
+            return
+
+        @pl.when(relay_share > detours.index(c))
         def _():
             detour_copies[c].wait_recv()
             forward_copies[c].start()
@@ -248,7 +309,7 @@
         [
             vertical(
                 side,
-                j,
+                min(j, 2) // 2,
                 previous.at[raw, pl.ds((layers - 1, 0)[side], 1), :],
                 first.at[span, pl.ds(far_layer[side], 1), body_cols],
             )
@@ -260,7 +321,7 @@
         [
             vertical(
                 side,
-                3 + j,
+                2 + min(j, 2) // 2,
                 second.at[span, pl.ds(own_layer[side], 1), body_cols],
                 second.at[span, pl.ds(far_layer[side], 1), body_cols],
             )
@@ -268,12 +329,20 @@
         ]
         for j, span in enumerate(spans)
     ]
+
+    def edge_layers(buffer, slot):
+        pair_span = pl.ds(1, 2)
+        return [
+            vertical(side, slot, *[buffer.at[pair_span, pl.ds(far_layer[side], 1), body_cols]] * 2)
+            for side in (0, 1)
+        ]
+
     sum_copies = [
         remote(
             sums,
             others.at[k - 1],
-            sum_send.at[k - 1],
-            sum_recv.at[k - 1],
+            sum_send.at[0],
+            sum_recv.at[0],
             {"depth": lax.rem(depth + k, depths)},
         )
         for k in range(1, depths)
@@ -287,17 +356,18 @@
         for side in (0, 1):
             pl.when(depth_recvs[side])(group[side].wait_recv)
 
-    def send(c):
-        send_outer(c)
-        partner_copies[c].start()
-
     with jax.named_scope("p02_sends"):
+        local_surface.wait()
         for side in (0, 1):
             pl.when(lat_sends[side])(surf_copies[side].start)
-        send(0)
         for group in raw_layers[:2]:
             start_layers(group)
-        send(1)
+        for c in range(RAW[OUTER]):
+            send_detour(c)
+        for c in range(RAW[PARTNER]):
+            partner_copies[c].start()
+        for c in range(RAW[OUTER]):
+            send_direct(c)
         start_layers(raw_layers[2])
 
     zero_tile = jnp.zeros((layers, PAD), jnp.float32)
@@ -325,7 +395,7 @@
             theirs[OUTER] = jnp.zeros((layers, columns), jnp.float32)
 
     with jax.named_scope("p04_waitsurf"):
-        for copy in locals_[:4]:
+        for copy in local_inputs:
             copy.wait()
         for side in (0, 1):
             pl.when(lat_recvs[side])(surf_copies[side].wait_recv)
@@ -353,9 +423,8 @@
     with jax.named_scope("p05_advect"):
         lax.fori_loop(0, steps, advect, 0)
     with jax.named_scope("p06_sends"):
-        for side in (0, 1):
-            pl.when(lat_sends[side])(shift_copies[side].start)
-        locals_[4].wait()
+        send_shift()
+        local_mesh.wait()
 
     def profile_of(index):
         return (total_layers - index).astype(jnp.float32) / total_layers
@@ -461,11 +530,10 @@
     with jax.named_scope("p07_widen"):
         over(1, 2, widen)
         over(rows - 1, 2, widen)
-        send(2)
-        send(3)
+        for c in range(RAW[PARTNER], CHUNKS):
+            partner_copies[c].start()
     with jax.named_scope("p08_waitraw"):
-        for group in raw_layers[:2]:
-            wait_layers(group)
+        wait_layers(edge_layers(first, 0))
     with jax.named_scope("p09_partial"):
         for flow in (OUTER, PARTNER):
             for step in range(steps):
@@ -474,61 +542,68 @@
         forward(0)
     with jax.named_scope("p11_widen"):
         over(3, rows - 4, widen)
-        send(4)
+        for c in range(CHUNKS, 2 * CHUNKS):
+            send_detour(c)
+        partner_copies[CHUNKS].start()
     with jax.named_scope("p12_waitraw"):
         wait_layers(raw_layers[2])
     middle_row = rows // 2 + 1
     with jax.named_scope("p13_sweep1"):
         over(2, middle_row - 2, sweep_once)
     with jax.named_scope("p14_fwd1"):
-        send(5)
+        partner_copies[CHUNKS + 1].start()
+        for c in (CHUNKS, CHUNKS + 1):
+            send_direct(c)
         forward(1)
+        forward(2)
     with jax.named_scope("p15_sweep1"):
         over(middle_row, rows - middle_row, sweep_once)
         start_layers(later_layers[2])
-    with jax.named_scope("p16_fwd2"):
-        send(6)
-        send(7)
-        forward(2)
+    with jax.named_scope("p16_fwd3"):
+        for c in range(CHUNKS + 2, 2 * CHUNKS):
+            partner_copies[c].start()
+            send_direct(c)
+        forward(3)
+    with jax.named_scope("p16_fwds"):
+        pl.when(has_beyond)(forward_shift)
     with jax.named_scope("p17_waitshift"):
-        for side in (0, 1):
-            pl.when(lat_recvs[side])(shift_copies[side].wait_recv)
-    for k in range(CHUNKS):
-        if k == CHUNKS - 1:
-            with jax.named_scope("p18_fwd3"):
-                forward(3)
-        for flow in (PARTNER, OUTER):
-
-            def arrive(flow=flow, k=k):
-                (partner_copies, outward_copies)[flow][k].wait_recv()
-                for j in range(per_piece if k < RAW else 0):
-                    widen(halos[flow], k * piece + j * WIDTH)
-
-            with jax.named_scope(f"p18_{k}{'po'[flow]}"):
-                if flow == PARTNER:
-                    arrive()
-                else:
-                    pl.when(has_outer)(arrive)
-            for j in range(per_piece):
-                complete(flow, k * piece + j * WIDTH)
+        shift_partner[0].wait_recv()
+        pl.when(has_outer)(shift_forward[0].wait_recv)
+    for flow in (PARTNER, OUTER):
+
+        def arrive(flow=flow):
+            whole_plane(flow).wait_recv()
+            for step in range(RAW[flow] * per_piece):
+                widen(halos[flow], step * WIDTH)
+
+        with jax.named_scope(f"p18_{flow}{'po'[flow]}"):
+            if flow == PARTNER:
+                arrive()
+            else:
+                pl.when(has_outer)(arrive)
+            for step in range(steps):
+                complete(flow, step * WIDTH)
     with jax.named_scope("p19_edges"):
         for j in (0, 1):
             start_layers(later_layers[j])
     with jax.named_scope("p20_waitlater"):
         wait_layers(later_layers[2])
     with jax.named_scope("p22_sweep2"):
-        over(2, rows - 2, sweep_twice)
+        over(2, middle_row - 2, sweep_twice)
+        over(middle_row, rows - middle_row, sweep_twice)
     with jax.named_scope("p23_waitlater"):
-        for j in (0, 1):
-            wait_layers(later_layers[j])
+        forward(CHUNKS)
+        forward(CHUNKS + 1)
+        wait_layers(edge_layers(second, 2))
     with jax.named_scope("p24_prepare"):
         for flow in (PARTNER, OUTER):
             for step in range(steps):
                 prepare(flow, step * WIDTH)
+        for c in range(CHUNKS + 2, 2 * CHUNKS):
+            forward(c)
 
     for k in range(CHUNKS):
         with jax.named_scope(f"p25_finish{k}"):
-            forward(CHUNKS + k)
             for flow in (PARTNER, OUTER):
                 if flow == PARTNER:
                     partner_copies[CHUNKS + k].wait_recv()
@@ -540,20 +615,27 @@
     sums[...] = jnp.sum(squares[...], axis=1)
     for copy in sum_copies:
         copy.start()
+    shift_partner[0].wait_send()
+    pl.when(has_outer)(shift_detour[0].wait_send)
+    pl.when(has_beyond)(shift_forward[0].wait_send)
     for side in (0, 1):
-        for copy in (surf_copies[side], shift_copies[side]):
-            pl.when(lat_sends[side])(copy.wait_send)
-        for group in raw_layers + later_layers:
-            pl.when(depth_sends[side])(group[side].wait_send)
-    for c in planes:
-        partner_copies[c].wait_send()
-        pl.when(has_outer)(outward_copies[c].wait_send)
-        pl.when(relay_share > c)(forward_copies[c].wait_send)
+        pl.when(lat_sends[side])(surf_copies[side].wait_send)
+        sent = first.at[pl.ds(1, rows), pl.ds(TILE, 2), body_cols]
+        pl.when(depth_sends[side])(vertical(side, 0, sent, sent).wait_send)
+
+    def sent_planes(flow):
+        return remote(mine, mine, plane_send.at[flow], plane_recv.at[flow, 0], lat_id(partner))
+
+    sent_planes(PARTNER).wait_send()
+    pl.when(has_outer)(sent_planes(OUTER).wait_send)
+    for count in sorted({(2 * CHUNKS * k) // pairs for k in range(1, pairs)} - {0}):
+        passed = relay.at[pl.ds(0, count)]
+        whole = remote(passed, passed, forward_send.at[0], relay_recv.at[0], lat_id(beyond))
+        pl.when(relay_share == count)(whole.wait_send)
     with jax.named_scope("p27_waitsums"):
-        for copy in sum_copies:
-            copy.wait_recv()
-        for copy in sum_copies:
-            copy.wait_send()
+        if depths > 1:
+            whole = remote(others, others, sum_send.at[0], sum_recv.at[0], {"depth": depth})
+            whole.wait()
     with jax.named_scope("p28_total"):
         total = sums[...]
         for k in range(depths - 1):
@@ -589,6 +671,7 @@
         anywhere = pl.BlockSpec(memory_space=pltpu.HBM)
         f32 = jnp.float32
         others = max(depths - 1, 1)
+        most = max((2 * CHUNKS * (lats // 2 - 1)) // (lats // 2), 1)
         dma = pltpu.SemaphoreType.DMA
         held = [
             pltpu.with_memory_space_constraint(value, pltpu.HBM)
@@ -613,21 +696,24 @@
                 pltpu.VMEM((rows + 2, layers + 2 * TILE, wide), f32),
                 pltpu.VMEM((2, layers, columns), f32),
                 pltpu.VMEM((2, layers, columns), f32),
-                pltpu.VMEM((2 * CHUNKS, layers, columns // CHUNKS), f32),
+                pltpu.VMEM((most, layers, columns // CHUNKS), f32),
+                pltpu.VMEM((1, RAW[OUTER] * (columns // CHUNKS)), f32),
                 pltpu.VMEM((rows, TILE, PAD), f32),
                 pltpu.VMEM((rows, PAD), f32),
                 pltpu.VMEM((others, rows, PAD), f32),
                 dma((5,)),
-                dma((2, 2)),
-                dma((2, 2)),
-                dma((2, 2 * CHUNKS)),
-                dma((2, 2 * CHUNKS)),
-                dma((2 * CHUNKS,)),
-                dma((2 * CHUNKS,)),
-                dma((2, 6)),
-                dma((2, 6)),
-                dma((others,)),
-                dma((others,)),
+                dma((2,)),
+                dma((2,)),
+                dma((3,)),
+                dma((3,)),
+                dma((2,)),
+                dma((2, 1 + CHUNKS)),
+                dma((most,)),
+                dma((1,)),
+                dma((2,)),
+                dma((2, 4)),
+                dma((1,)),
+                dma((1,)),
             ],
             compiler_params=pltpu.CompilerParams(
                 collective_id=0, has_side_effects=True, vmem_limit_bytes=56 * 1024 * 1024

time: 33.3 us -> 32.8 us (0.985)
  no operation moved by 1% of the time
where the time goes in v2:
time: 32.8 us; the launch traced here: 32.6 us
  Pallas kernels  32 us (98%)
  between operations  0.64 us (2%)
    pallas_call x1, Pallas kernels, per_device(): pl.pallas_call(functools.partial(kernel, lats, depths), out_shape=(pltpu....  29.9 us
    pallas_call x1, Pallas kernels, per_device(): pl.pallas_call(functools.partial(deliver, layers * depths * columns), out...  2.11 us

profile of v2, /device:TPU:0, one launch (start us, length us, event | category | flops | bytes accessed | tf_op | source)
XLA Modules:
  0.0 32.6 jit_solution(14311849120276301261)
XLA Ops:
  0.6 29.9 %advect_and_relax.1 = (f32[16,4096]{1,0:T(8,128)S(1)}, f32[16,16,4096]{2,1,0:T(8,128)S(1)}, f32[16,128]{1,0:T(8,128)S(1)}) custom-call(f32[16,4096]{1,0:T(8,128)} %surface.1, f32[2,16,4096]{2,1,0:T(8,128)} %velocity.1, s32[16,4096]{1,0:T(8,128)} %block_map.1, s32[16,4096]{1,0:T(8,128)} %free_flags.1, f32[16]{0:T(128)} %rates.1, f32[16,16,4096]{2,1,0:T(8,128)} %previous.1), custom_call_target="tpu_custom_call" | custom-call | tf_op jit(solution)/shard_map/advect_and_relax/pallas_call | solution.py:680
  30.5 2.1 %deliver.1 = (f32[16,4096]{1,0:T(8,128)}, f32[16,16,4096]{2,1,0:T(8,128)}, f32[16]{0:T(128)}) custom-call(f32[16,4096]{1,0:T(8,128)S(1)} %get-tuple-element.6.surface_in, f32[16,16,4096]{2,1,0:T(8,128)S(1)} %get-tuple-element.7.field_in, f32[16,128]{1,0:T(8,128)S(1)} %get-tuple-element.8.total), custom_call_target="tpu_custom_call" | custom-call | tf_op jit(solution)/shard_map/deliver/pallas_call | solution.py:724

commit v3 on v2

--- a/solution.py
+++ b/solution.py
@@ -16,7 +16,7 @@
 TILE = 8
 WIDTH = 1024
 CHUNKS = 4
-RAW = (2, CHUNKS)
+RAW = (2, 2)
 PARTNER, OUTER = 0, 1
 
 
@@ -34,7 +34,7 @@
     velocity,
     block_map,
     free_flags,
-    rates,
+    block_rates,
     previous,
     new_surface,
     field,
@@ -43,6 +43,7 @@
     vel,
     blocks,
     flags,
+    rates,
     shift,
     first,
     second,
@@ -71,7 +72,7 @@
     lat = lax.axis_index("lat")
     depth = lax.axis_index("depth")
     total_layers = layers * depths
-    blocks_count = rates.shape[0]
+    blocks_count = block_rates.shape[0]
     steps = columns // WIDTH
     piece = columns // CHUNKS
     per_piece = piece // WIDTH
@@ -90,7 +91,8 @@
     has_outer = jnp.logical_and(outward >= 0, outward < lats)
     has_beyond = jnp.logical_and(beyond >= 0, beyond < lats)
     down_share = (2 * CHUNKS * pair) // pairs
-    up_share = (2 * CHUNKS * (pairs - 1 - pair)) // pairs
+    up_share = (2 * CHUNKS * (pairs - 1 - pair)) // pairs - lax.rem(depth, 2)
+    up_share = jnp.maximum(up_share, 0)
     own_share = jnp.where(odd == 0, down_share, up_share)
     relay_share = jnp.where(odd == 0, up_share, down_share)
     low_side, high_side = odd, 1 - odd
@@ -105,6 +107,7 @@
         pltpu.make_async_copy(velocity, vel, local_sem.at[1]),
         pltpu.make_async_copy(block_map, blocks, local_sem.at[2]),
         pltpu.make_async_copy(free_flags, flags, local_sem.at[3]),
+        pltpu.make_async_copy(block_rates, rates, local_sem.at[5]),
     ]
     local_mesh = pltpu.make_async_copy(
         previous, first.at[pl.ds(1, rows), body_layers, body_cols], local_sem.at[4]
@@ -124,7 +127,7 @@
     pl.when(has_outer)(lambda: greet(lat_id(behind)))
     for k in range(1, depths):
         greet({"depth": lax.rem(depth + k, depths)})
-    for copy in [local_surface, *local_inputs, local_mesh]:
+    for copy in [local_surface]:
         copy.start()
     peers = depths + 2 * has_outer.astype(jnp.int32) + has_beyond.astype(jnp.int32)
     with jax.named_scope("p01_barrier"):
@@ -370,6 +373,8 @@
             send_direct(c)
         start_layers(raw_layers[2])
 
+    for copy in [*local_inputs, local_mesh]:
+        copy.start()
     zero_tile = jnp.zeros((layers, PAD), jnp.float32)
 
     def clear_pads(r, carry):
@@ -530,8 +535,12 @@
     with jax.named_scope("p07_widen"):
         over(1, 2, widen)
         over(rows - 1, 2, widen)
+        for c in range(RAW[OUTER], CHUNKS):
+            send_detour(c)
         for c in range(RAW[PARTNER], CHUNKS):
             partner_copies[c].start()
+        for c in range(RAW[OUTER], CHUNKS):
+            send_direct(c)
     with jax.named_scope("p08_waitraw"):
         wait_layers(edge_layers(first, 0))
     with jax.named_scope("p09_partial"):
@@ -555,7 +564,6 @@
         for c in (CHUNKS, CHUNKS + 1):
             send_direct(c)
         forward(1)
-        forward(2)
     with jax.named_scope("p15_sweep1"):
         over(middle_row, rows - middle_row, sweep_once)
         start_layers(later_layers[2])
@@ -563,6 +571,7 @@
         for c in range(CHUNKS + 2, 2 * CHUNKS):
             partner_copies[c].start()
             send_direct(c)
+        forward(2)
         forward(3)
     with jax.named_scope("p16_fwds"):
         pl.when(has_beyond)(forward_shift)
@@ -628,7 +637,7 @@
 
     sent_planes(PARTNER).wait_send()
     pl.when(has_outer)(sent_planes(OUTER).wait_send)
-    for count in sorted({(2 * CHUNKS * k) // pairs for k in range(1, pairs)} - {0}):
+    for count in range(1, most + 1):
         passed = relay.at[pl.ds(0, count)]
         whole = remote(passed, passed, forward_send.at[0], relay_recv.at[0], lat_id(beyond))
         pl.when(relay_share == count)(whole.wait_send)
@@ -675,7 +684,7 @@
         dma = pltpu.SemaphoreType.DMA
         held = [
             pltpu.with_memory_space_constraint(value, pltpu.HBM)
-            for value in (surface, velocity, block_map, free_flags, previous_mesh)
+            for value in (surface, velocity, block_map, free_flags, block_rates, previous_mesh)
         ]
         results = pl.pallas_call(
             functools.partial(kernel, lats, depths),
@@ -684,13 +693,14 @@
                 pltpu.VMEM(previous_mesh.shape, f32),
                 pltpu.VMEM((rows, PAD), f32),
             ),
-            in_specs=[anywhere] * 4 + [pl.BlockSpec(memory_space=pltpu.SMEM), anywhere],
+            in_specs=[anywhere] * 6,
             out_specs=(pl.BlockSpec(memory_space=pltpu.VMEM),) * 3,
             scratch_shapes=[
                 pltpu.VMEM((rows + 2 * TILE, wide), f32),
                 pltpu.VMEM(velocity.shape, f32),
                 pltpu.VMEM(block_map.shape, jnp.int32),
                 pltpu.VMEM(free_flags.shape, jnp.int32),
+                pltpu.SMEM(block_rates.shape, f32),
                 pltpu.VMEM((rows + 2 * TILE, columns), f32),
                 pltpu.VMEM((rows + 2, layers + 2 * TILE, wide), f32),
                 pltpu.VMEM((rows + 2, layers + 2 * TILE, wide), f32),
@@ -701,7 +711,7 @@
                 pltpu.VMEM((rows, TILE, PAD), f32),
                 pltpu.VMEM((rows, PAD), f32),
                 pltpu.VMEM((others, rows, PAD), f32),
-                dma((5,)),
+                dma((6,)),
                 dma((2,)),
                 dma((2,)),
                 dma((3,)),
@@ -719,7 +729,7 @@
                 collective_id=0, has_side_effects=True, vmem_limit_bytes=56 * 1024 * 1024
             ),
             name="advect_and_relax",
-        )(*held[:4], block_rates, held[4])
+        )(*held)
         resident = [pltpu.with_memory_space_constraint(value, pltpu.VMEM) for value in results]
         new_surface, field, norm = pl.pallas_call(
             functools.partial(deliver, layers * depths * columns),

time: 32.8 us -> 31.3 us (0.954)
  Pallas kernels: 32 us -> 30.5 us
    pallas_call x1, Pallas kernels: 29.9 us -> 28.4 us  [per_device(): pl.pallas_call(functools.partial(kernel, lats, depths), out_shape=(pltpu....]
where the time goes in v3:
time: 31.3 us; the launch traced here: 31.1 us
  Pallas kernels  30.5 us (97%)
  between operations  0.64 us (2%)
    pallas_call x1, Pallas kernels, per_device(): pl.pallas_call(functools.partial(kernel, lats, depths), out_shape=(pltpu....  28.4 us
    pallas_call x1, Pallas kernels, per_device(): pl.pallas_call(functools.partial(deliver, layers * depths * columns), out...  2.11 us

profile of v3, /device:TPU:0, one launch (start us, length us, event | category | flops | bytes accessed | tf_op | source)
XLA Modules:
  0.0 31.1 jit_solution(14046869771204931691)
XLA Ops:
  0.6 28.4 %advect_and_relax.1 = (f32[16,4096]{1,0:T(8,128)S(1)}, f32[16,16,4096]{2,1,0:T(8,128)S(1)}, f32[16,128]{1,0:T(8,128)S(1)}) custom-call(f32[16,4096]{1,0:T(8,128)} %surface.1, f32[2,16,4096]{2,1,0:T(8,128)} %velocity.1, s32[16,4096]{1,0:T(8,128)} %block_map.1, s32[16,4096]{1,0:T(8,128)} %free_flags.1, f32[16]{0:T(128)} %block_rates.1, f32[16,16,4096]{2,1,0:T(8,128)} %previous.1), custom_call_target="tpu_custom_call" | custom-call | tf_op jit(solution)/shard_map/advect_and_relax/pallas_call | solution.py:689
  29.0 2.1 %deliver.1 = (f32[16,4096]{1,0:T(8,128)}, f32[16,16,4096]{2,1,0:T(8,128)}, f32[16]{0:T(128)}) custom-call(f32[16,4096]{1,0:T(8,128)S(1)} %get-tuple-element.6.surface_in, f32[16,16,4096]{2,1,0:T(8,128)S(1)} %get-tuple-element.7.field_in, f32[16,128]{1,0:T(8,128)S(1)} %get-tuple-element.8.total), custom_call_target="tpu_custom_call" | custom-call | tf_op jit(solution)/shard_map/deliver/pallas_call | solution.py:734

commit v4 on v3

--- a/solution.py
+++ b/solution.py
@@ -54,6 +54,8 @@
     squares,
     sums,
     others,
+    last,
+    last_others,
     local_sem,
     near_send,
     near_recv,
@@ -240,7 +242,7 @@
     detours = order[:most]
 
     def landed(flow, c):
-        return plane_recv.at[flow, max(c - CHUNKS + 1, 0)]
+        return plane_recv.at[flow if c < CHUNKS else 2 + c - CHUNKS]
 
     partner_copies = [
         remote(
@@ -285,7 +287,7 @@
 
     def whole_plane(flow):
         whole = first.at[halos[flow], body_layers, body_cols]
-        return remote(whole, whole, plane_send.at[flow], plane_recv.at[flow, 0], lat_id(partner))
+        return remote(whole, whole, plane_send.at[flow], plane_recv.at[flow], lat_id(partner))
 
     def send_detour(c):
         if c in detour_copies:
@@ -340,16 +342,23 @@
             for side in (0, 1)
         ]
 
-    sum_copies = [
-        remote(
-            sums,
-            others.at[k - 1],
-            sum_send.at[0],
-            sum_recv.at[0],
-            {"depth": lax.rem(depth + k, depths)},
-        )
-        for k in range(1, depths)
-    ]
+    sum_copies, last_copies = [
+        [
+            remote(
+                src,
+                dst.at[k - 1],
+                sum_send.at[kind],
+                sum_recv.at[kind],
+                {"depth": lax.rem(depth + k, depths)},
+            )
+            for k in range(1, depths)
+        ]
+        for kind, (src, dst) in enumerate(((sums, others), (last, last_others)))
+    ]
+
+    def settle(kind, buffer):
+        if depths > 1:
+            remote(buffer, buffer, sum_send.at[kind], sum_recv.at[kind], {"depth": depth}).wait()
 
     def start_layers(group):
         for side in (0, 1):
@@ -600,6 +609,9 @@
     with jax.named_scope("p22_sweep2"):
         over(2, middle_row - 2, sweep_twice)
         over(middle_row, rows - middle_row, sweep_twice)
+        sums[...] = jnp.sum(squares[...], axis=1)
+        for copy in sum_copies:
+            copy.start()
     with jax.named_scope("p23_waitlater"):
         forward(CHUNKS)
         forward(CHUNKS + 1)
@@ -613,17 +625,26 @@
 
     for k in range(CHUNKS):
         with jax.named_scope(f"p25_finish{k}"):
+            both = theirs.at[:, :, piece_cols(k)]
+            arrivals = remote(
+                both, both, plane_send.at[PARTNER], plane_recv.at[2 + k], lat_id(partner)
+            )
+            pl.when(has_outer)(arrivals.wait_recv)
+            pl.when(jnp.logical_not(has_outer))(partner_copies[CHUNKS + k].wait_recv)
             for flow in (PARTNER, OUTER):
-                if flow == PARTNER:
-                    partner_copies[CHUNKS + k].wait_recv()
-                else:
-                    pl.when(has_outer)(outward_copies[CHUNKS + k].wait_recv)
                 for j in range(per_piece):
                     finish(flow, k * piece + j * WIDTH)
 
-    sums[...] = jnp.sum(squares[...], axis=1)
-    for copy in sum_copies:
+    for flow in (PARTNER, OUTER):
+        edge_squares = jnp.sum(squares[edges[flow] - 1], axis=0, keepdims=True)
+        last[:, pl.ds(flow * PAD, PAD)] = edge_squares
+    for copy in last_copies:
         copy.start()
+    settle(0, others)
+    total = sums[...]
+    for k in range(depths - 1):
+        total = total + others[k]
+    norm[...] = total
     shift_partner[0].wait_send()
     pl.when(has_outer)(shift_detour[0].wait_send)
     pl.when(has_beyond)(shift_forward[0].wait_send)
@@ -633,7 +654,7 @@
         pl.when(depth_sends[side])(vertical(side, 0, sent, sent).wait_send)
 
     def sent_planes(flow):
-        return remote(mine, mine, plane_send.at[flow], plane_recv.at[flow, 0], lat_id(partner))
+        return remote(mine, mine, plane_send.at[flow], plane_recv.at[flow], lat_id(partner))
 
     sent_planes(PARTNER).wait_send()
     pl.when(has_outer)(sent_planes(OUTER).wait_send)
@@ -642,14 +663,13 @@
         whole = remote(passed, passed, forward_send.at[0], relay_recv.at[0], lat_id(beyond))
         pl.when(relay_share == count)(whole.wait_send)
     with jax.named_scope("p27_waitsums"):
-        if depths > 1:
-            whole = remote(others, others, sum_send.at[0], sum_recv.at[0], {"depth": depth})
-            whole.wait()
+        settle(1, last_others)
     with jax.named_scope("p28_total"):
-        total = sums[...]
+        total = last[...]
         for k in range(depths - 1):
-            total = total + others[k]
-        norm[...] = total
+            total = total + last_others[k]
+        for flow in (PARTNER, OUTER):
+            norm[pl.ds(edges[flow] - 1, 1), :] = total[:, flow * PAD : (flow + 1) * PAD]
 
 
 def deliver(count, surface_in, field_in, total, surface_out, field_out, norm_out, packed, sem):
@@ -711,19 +731,21 @@
                 pltpu.VMEM((rows, TILE, PAD), f32),
                 pltpu.VMEM((rows, PAD), f32),
                 pltpu.VMEM((others, rows, PAD), f32),
+                pltpu.VMEM((1, 2 * PAD), f32),
+                pltpu.VMEM((others, 1, 2 * PAD), f32),
                 dma((6,)),
                 dma((2,)),
                 dma((2,)),
                 dma((3,)),
                 dma((3,)),
                 dma((2,)),
-                dma((2, 1 + CHUNKS)),
+                dma((2 + CHUNKS,)),
                 dma((most,)),
                 dma((1,)),
                 dma((2,)),
                 dma((2, 4)),
-                dma((1,)),
-                dma((1,)),
+                dma((2,)),
+                dma((2,)),
             ],
             compiler_params=pltpu.CompilerParams(
                 collective_id=0, has_side_effects=True, vmem_limit_bytes=56 * 1024 * 1024

time: 31.3 us -> 31.2 us (level)
  no operation moved by 1% of the time
where the time goes in v4:
time: 31.2 us; the launch traced here: 31 us
  Pallas kernels  30.4 us (97%)
  between operations  0.64 us (2%)
    pallas_call x1, Pallas kernels, per_device(): pl.pallas_call(functools.partial(kernel, lats, depths), out_shape=(pltpu....  28.3 us
    pallas_call x1, Pallas kernels, per_device(): pl.pallas_call(functools.partial(deliver, layers * depths * columns), out...  2.11 us

profile of v4, /device:TPU:0, one launch (start us, length us, event | category | flops | bytes accessed | tf_op | source)
XLA Modules:
  0.0 31.0 jit_solution(8362685520347288562)
XLA Ops:
  0.6 28.3 %advect_and_relax.1 = (f32[16,4096]{1,0:T(8,128)S(1)}, f32[16,16,4096]{2,1,0:T(8,128)S(1)}, f32[16,128]{1,0:T(8,128)S(1)}) custom-call(f32[16,4096]{1,0:T(8,128)} %surface.1, f32[2,16,4096]{2,1,0:T(8,128)} %velocity.1, s32[16,4096]{1,0:T(8,128)} %block_map.1, s32[16,4096]{1,0:T(8,128)} %free_flags.1, f32[16]{0:T(128)} %block_rates.1, f32[16,16,4096]{2,1,0:T(8,128)} %previous.1), custom_call_target="tpu_custom_call" | custom-call | tf_op jit(solution)/shard_map/advect_and_relax/pallas_call | solution.py:709
  28.9 2.1 %deliver.1 = (f32[16,4096]{1,0:T(8,128)}, f32[16,16,4096]{2,1,0:T(8,128)}, f32[16]{0:T(128)}) custom-call(f32[16,4096]{1,0:T(8,128)S(1)} %get-tuple-element.6.surface_in, f32[16,16,4096]{2,1,0:T(8,128)S(1)} %get-tuple-element.7.field_in, f32[16,128]{1,0:T(8,128)S(1)} %get-tuple-element.8.total), custom_call_target="tpu_custom_call" | custom-call | tf_op jit(solution)/shard_map/deliver/pallas_call | solution.py:756

commit v5 on v4

--- a/solution.py
+++ b/solution.py
@@ -372,12 +372,12 @@
         local_surface.wait()
         for side in (0, 1):
             pl.when(lat_sends[side])(surf_copies[side].start)
-        for group in raw_layers[:2]:
-            start_layers(group)
         for c in range(RAW[OUTER]):
             send_detour(c)
         for c in range(RAW[PARTNER]):
             partner_copies[c].start()
+        for group in raw_layers[:2]:
+            start_layers(group)
         for c in range(RAW[OUTER]):
             send_direct(c)
         start_layers(raw_layers[2])

time: 31.2 us -> 31.2 us (level)
  no operation moved by 1% of the time
where the time goes in v5:
time: 31.2 us; the launch traced here: 31 us
  Pallas kernels  30.4 us (97%)
  between operations  0.64 us (2%)
    pallas_call x1, Pallas kernels, per_device(): pl.pallas_call(functools.partial(kernel, lats, depths), out_shape=(pltpu....  28.3 us
    pallas_call x1, Pallas kernels, per_device(): pl.pallas_call(functools.partial(deliver, layers * depths * columns), out...  2.11 us

profile of v5, /device:TPU:0, one launch (start us, length us, event | category | flops | bytes accessed | tf_op | source)
XLA Modules:
  0.0 31.0 jit_solution(18173664045098575699)
XLA Ops:
  0.6 28.3 %advect_and_relax.1 = (f32[16,4096]{1,0:T(8,128)S(1)}, f32[16,16,4096]{2,1,0:T(8,128)S(1)}, f32[16,128]{1,0:T(8,128)S(1)}) custom-call(f32[16,4096]{1,0:T(8,128)} %surface.1, f32[2,16,4096]{2,1,0:T(8,128)} %velocity.1, s32[16,4096]{1,0:T(8,128)} %block_map.1, s32[16,4096]{1,0:T(8,128)} %free_flags.1, f32[16]{0:T(128)} %block_rates.1, f32[16,16,4096]{2,1,0:T(8,128)} %previous.1), custom_call_target="tpu_custom_call" | custom-call | tf_op jit(solution)/shard_map/advect_and_relax/pallas_call | solution.py:709
  28.9 2.1 %deliver.1 = (f32[16,4096]{1,0:T(8,128)}, f32[16,16,4096]{2,1,0:T(8,128)}, f32[16]{0:T(128)}) custom-call(f32[16,4096]{1,0:T(8,128)S(1)} %get-tuple-element.6.surface_in, f32[16,16,4096]{2,1,0:T(8,128)S(1)} %get-tuple-element.7.field_in, f32[16,128]{1,0:T(8,128)S(1)} %get-tuple-element.8.total), custom_call_target="tpu_custom_call" | custom-call | tf_op jit(solution)/shard_map/deliver/pallas_call | solution.py:756
